TPU v7x, 32 devices: a whole 2x2x4 slice. The times are simulated.
32 devices in a mesh: radar: 4 (over x, core), tile: 8 (over z, y).
Axes of the slice: x: 2, y: 2, z: 4, core: 2. Of those that a mesh axis runs over, the one named last changes fastest.
Arguments:
- background: float32 [3, 128, 32, 1024], P(None, 'tile', None, 'radar'), may hold values from -6 to 6
- interp: bfloat16 [2048, 128, 128], P(('radar', 'tile')), may hold values from -0.5 to 0.5
- beam: bfloat16 [2048, 3, 128], P(('radar', 'tile')), may hold values from -1 to 1
- observed: bfloat16 [2048, 128], P(('radar', 'tile')), may hold values from -6 to 6
- cell_block: int32 [2048], P(('radar', 'tile')), may hold values from 0 to 1023
- sweep_count: int32 [32, 32], P(('radar', 'tile')), may hold values from 0 to 2, as said below
Outputs:
- wind_field: float32 [3, 128, 32, 1024], P(None, 'tile', None, 'radar')
- strain: float32 [6, 128, 32, 1024], P(None, 'tile', None, 'radar')
- cost_trace: float32 [2], replicated
Inputs may be any that keep to these rules, and one draw needn't show every extreme that they name: `cell_block`: the cell block, within the owner's 16 x 32 x 256 cells of one component, read by a slot. `sweep_count`: every source device has an owning device to which all 2 of its slots are live.
All inputs are finite; a program needn't handle non-finite values.
Results may differ from a plain program's by a relative error of at most 0.0014.
Values may be sent and summed in bfloat16 or wider, within the bound.
No kernel may reach another device: no remote copies, remote signals or barrier semaphores. Data moves between devices by JAX's collectives and lax.ppermute only.
A program may use at most 64 MiB of HBM per device.

v0:
```python
import jax
import jax.numpy as jnp
from jax import lax
from jax.sharding import PartitionSpec as P

ITERS = 2
BACKGROUND_WEIGHT = 0.5
DIVERGENCE_WEIGHT = 1.0
STEP_LENGTH = 0.3
EPSILON = 1e-06


def with_halo(x, sides, width):
    for axis, dim in sides:
        size, length = (lax.axis_size(axis), x.shape[dim])
        up = [(i, (i + 1) % size) for i in range(size - 1)]
        down = [(j, i) for i, j in up]
        last = lax.slice_in_dim(x, length - width, length, axis=dim)
        first = lax.slice_in_dim(x, 0, width, axis=dim)
        before = lax.ppermute(last, axis, up)
        after = lax.ppermute(first, axis, down)
        x = jnp.concatenate([before, x, after], axis=dim)
    return x


def vertical_diff(values):
    padded = jnp.pad(values, ((0, 0), (1, 1), (0, 0)))
    return 0.5 * (padded[:, 2:, :] - padded[:, :-2, :])


def along_x(values):
    return 0.5 * (values[2:, :, 1:-1] - values[:-2, :, 1:-1])


def along_y(values):
    return 0.5 * (values[1:-1, :, 2:] - values[1:-1, :, :-2])


def along_z(values):
    return vertical_diff(values[1:-1, :, 1:-1])


def observe(cell_rows, weights, beam_rows, looked, alive_mask):
    projected = jnp.einsum("knc,ngc->nkg", cell_rows, weights, preferred_element_type=jnp.float32)
    beam_values = beam_rows.astype(jnp.float32)
    radial = jnp.sum(beam_values * projected, axis=1)
    misfit = alive_mask[:, None] * (radial - looked.astype(jnp.float32))
    adjoint = (beam_values * misfit[:, None, :]).astype(jnp.bfloat16)
    returned = jnp.einsum("nkg,ngc->knc", adjoint, weights, preferred_element_type=jnp.float32)
    return (0.5 * jnp.sum(misfit * misfit), returned)


def spread_cycle(wind_field, tile_count, radar_count):
    width_x = wind_field.shape[1]
    width_y = wind_field.shape[3]
    rim = with_halo(wind_field, (("radar", 3), ("tile", 1)), 2)
    cycle = along_x(rim[0]) + along_y(rim[1]) + along_z(rim[2])
    row_place = lax.axis_index("tile") * width_x - 1 + jnp.arange(width_x + 2, dtype=jnp.int32)
    col_place = lax.axis_index("radar") * width_y - 1 + jnp.arange(width_y + 2, dtype=jnp.int32)
    row_inside = (row_place >= 0) & (row_place < width_x * tile_count)
    col_inside = (col_place >= 0) & (col_place < width_y * radar_count)
    inside = row_inside[:, None, None] & col_inside[None, None, :]
    cycle = jnp.where(inside, cycle, 0.0)
    spread = cycle[1:-1, :, 1:-1]
    push = jnp.stack([-along_x(cycle), -along_y(cycle), -vertical_diff(spread)])
    return (spread, push)


def shards(background, interp, beam, observed, cell_block, sweep_count):
    radar_count = lax.axis_size("radar")
    tile_count = lax.axis_size("tile")
    devices = radar_count * tile_count
    width_x = background.shape[1]
    levels = background.shape[2]
    width_y = background.shape[3]
    slots = interp.shape[0] // devices
    gate_size = interp.shape[1]
    block_total = width_x * levels * width_y // gate_size
    total_cells = 3 * width_x * levels * width_y * devices
    total_gates = interp.shape[0] * devices * gate_size
    own_index = cell_block.reshape(devices, slots)
    own_alive = (
        jnp.arange(slots, dtype=jnp.int32)[None, :] < sweep_count.reshape(devices)[:, None]
    ).astype(jnp.int32)
    packed = jnp.stack([own_index, own_alive], 1)
    asked = lax.all_to_all(packed, ("radar", "tile"), split_axis=0, concat_axis=0, tiled=True)
    asked_index = asked[:, 0, :].reshape(-1)
    asked_alive = asked[:, 1, :].reshape(-1).astype(jnp.float32)
    got_weights, got_beam, got_looked = (
        lax.all_to_all(
            interp.reshape(devices, slots, gate_size, gate_size),
            ("radar", "tile"),
            split_axis=0,
            concat_axis=0,
            tiled=True,
        ),
        lax.all_to_all(
            beam.reshape(devices, slots, 3, gate_size),
            ("radar", "tile"),
            split_axis=0,
            concat_axis=0,
            tiled=True,
        ),
        lax.all_to_all(
            observed.reshape(devices, slots, gate_size),
            ("radar", "tile"),
            split_axis=0,
            concat_axis=0,
            tiled=True,
        ),
    )
    got_weights = got_weights.reshape(devices * slots, gate_size, gate_size)
    got_beam = got_beam.reshape(devices * slots, 3, gate_size)
    got_looked = got_looked.reshape(devices * slots, gate_size)
    wind_field = background
    trace = []
    for step_index in range(ITERS):
        flat = wind_field.reshape(3, block_total, gate_size)
        empty = jnp.zeros((3, block_total, gate_size), jnp.float32)
        chosen = flat[:, asked_index, :].astype(jnp.bfloat16)
        obs_cost, returned = observe(chosen, got_weights, got_beam, got_looked, asked_alive)
        obs_cost, obs_flat = (obs_cost, empty.at[:, asked_index, :].add(returned))
        obs_grad = obs_flat.reshape(wind_field.shape)
        spread, push = spread_cycle(wind_field, tile_count, radar_count)
        offset = wind_field - background
        gradient = obs_grad + BACKGROUND_WEIGHT * offset + DIVERGENCE_WEIGHT * push
        local_cost = (
            obs_cost
            + 0.5 * BACKGROUND_WEIGHT * jnp.sum(offset * offset)
            + 0.5 * DIVERGENCE_WEIGHT * jnp.sum(spread * spread)
        )
        cost_sum, square_sum = lax.psum(
            (local_cost, jnp.sum(gradient * gradient)), ("radar", "tile")
        )
        scale = jnp.sqrt(square_sum / total_cells + EPSILON)
        wind_field = wind_field - STEP_LENGTH * gradient / scale
        trace.append(cost_sum / total_gates)
    faces = with_halo(wind_field, (("radar", 3), ("tile", 1)), 1)
    east_wind, north_wind, upward_wind = (faces[0], faces[1], faces[2])
    strain = jnp.stack(
        [
            along_x(east_wind),
            along_y(north_wind),
            along_z(upward_wind),
            0.5 * (along_y(east_wind) + along_x(north_wind)),
            0.5 * (along_z(east_wind) + along_x(upward_wind)),
            0.5 * (along_z(north_wind) + along_y(upward_wind)),
        ]
    )
    return (wind_field, strain, jnp.stack(trace))


def solution(mesh):
    placed = (
        P(None, "tile", None, "radar"),
        P(("radar", "tile"), None, None),
        P(("radar", "tile"), None, None),
        P(("radar", "tile"), None),
        P(("radar", "tile")),
        P(("radar", "tile"), None),
    )
    return jax.shard_map(
        shards,
        mesh=mesh,
        in_specs=placed,
        out_specs=(P(None, "tile", None, "radar"), P(None, "tile", None, "radar"), P()),
        check_vma=False,
    )
```

profile of v0, /device:TPU:1, one launch (start us, length us, event | category | flops | bytes accessed | tf_op | source)
XLA Modules:
  0.0 292.6 jit_solution(12038039125268304084)
XLA Ops:
  2.8 7.1 %all-to-all-start = ((s32[32,2,2]{2,1,0:T(2,128)}), s32[32,2,2]{2,1,0:T(2,128)S(1)}, u32[]{:S(2)}, u32[]{:S(2)}) async-start(s32[32,2,2]{2,1,0:T(2,128)} %copy.109), calls=%async_computation | async-start | bytes 65536 | tf_op jit(solution)/shard_map/all_to_all | solution.py:86
  10.7 6.2 %all-to-all-done = s32[32,2,2]{2,1,0:T(2,128)S(1)} async-done(((s32[32,2,2]{2,1,0:T(2,128)}), s32[32,2,2]{2,1,0:T(2,128)S(1)}, u32[]{:S(2)}, u32[]{:S(2)}) %all-to-all-start) | async-done | bytes 544 | tf_op jit(solution)/shard_map/all_to_all | solution.py:86
  16.9 8.9 %all_to_all.20 = bf16[32,2,3,128]{3,1,2,0:T(2,128)(2,1)S(1)} all-to-all(bf16[32,2,3,128]{3,1,2,0:T(2,128)(2,1)S(1)} %copy.110), channel_id=1, replica_groups=mesh['radar'=4,'tile'=8] {'radar','tile'}, dimensions={0} | all-to-all | bytes 98304 | tf_op jit(solution)/shard_map/all_to_all | solution.py:97
  25.8 3.5 %all-to-all-start.2 = ((bf16[32,2,128,128]{3,2,1,0:T(8,128)(2,1)}), bf16[32,2,128,128]{3,2,1,0:T(8,128)(2,1)}, u32[]{:S(2)}, u32[]{:S(2)}) async-start(bf16[32,2,128,128]{3,2,1,0:T(8,128)(2,1)} %bitcast.87), calls=%async_computation.2 | async-start | bytes 4194304 | tf_op jit(solution)/shard_map/all_to_all | solution.py:90
  30.7 3.5 %collective-permute-start = (f32[3,16,32,2]{2,1,3,0:T(8,128)}, f32[3,16,32,2]{2,1,3,0:T(8,128)}, u32[]{:S(2)}, u32[]{:S(2)}) collective-permute-start(f32[3,16,32,2]{2,1,3,0:T(8,128)} %copy.136), channel_id=1, source_target_pairs={{0,8},{8,16},{16,24},{1,9},{9,17},{17,25},{2,10},{10,18},{18,26},{... | collective-permute-start | bytes 36872 | tf_op jit(solution)/shard_map/ppermute | solution.py:20
  44.6 3.4 %collective-permute-start.2 = (f32[3,2,32,260]{3,2,1,0:T(8,128)S(1)}, f32[3,2,32,260]{3,2,1,0:T(8,128)S(1)}, u32[]{:S(2)}, u32[]{:S(2)}) collective-permute-start(f32[3,2,32,260]{3,2,1,0:T(8,128)S(1)} %get-tuple-element.19), channel_id=1, source_target_pairs={{0,1},{1,2},{2,3},{3,4},{4,5},{5,6},{6,7},{8,9},{9,10},{10,11},{11... | collective-permute-start | bytes 599048 | tf_op jit(solution)/shard_map/ppermute | solution.py:20
  49.4 10.3 %collective-permute-done.2 = f32[3,2,32,260]{3,2,1,0:T(8,128)S(1)} collective-permute-done((f32[3,2,32,260]{3,2,1,0:T(8,128)S(1)}, f32[3,2,32,260]{3,2,1,0:T(8,128)S(1)}, u32[]{:S(2)}, u32[]{:S(2)}) %collective-permute-start.2) | collective-permute-done | bytes 199712 | tf_op jit(solution)/shard_map/ppermute | solution.py:20
  66.5 12.5 %all-to-all-done.2 = bf16[32,2,128,128]{3,2,1,0:T(8,128)(2,1)} async-done(((bf16[32,2,128,128]{3,2,1,0:T(8,128)(2,1)}), bf16[32,2,128,128]{3,2,1,0:T(8,128)(2,1)}, u32[]{:S(2)}, u32[]{:S(2)}) %all-to-all-start.2) | async-done | bytes 2097184 | tf_op jit(solution)/shard_map/all_to_all | solution.py:90
  79.0 13.4 %all-to-all-start.3 = ((bf16[32,2,128]{2,1,0:T(2,128)(2,1)}), bf16[32,2,128]{2,1,0:T(2,128)(2,1)S(1)}, u32[]{:S(2)}, u32[]{:S(2)}) async-start(bf16[32,2,128]{2,1,0:T(2,128)(2,1)} %bitcast.7), calls=%async_computation.3 | async-start | bytes 32768 | tf_op jit(solution)/shard_map/all_to_all | solution.py:104
  95.2 3.9 %all-to-all-done.3 = bf16[32,2,128]{2,1,0:T(2,128)(2,1)S(1)} async-done(((bf16[32,2,128]{2,1,0:T(2,128)(2,1)}), bf16[32,2,128]{2,1,0:T(2,128)(2,1)S(1)}, u32[]{:S(2)}, u32[]{:S(2)}) %all-to-all-start.3) | async-done | bytes 16416 | tf_op jit(solution)/shard_map/all_to_all | solution.py:104
  103.0 7.1 %scatter_fusion = f32[3,1024,128]{2,0,1:T(4,128)} fusion(f32[3,1024,128]{2,0,1:T(4,128)} %broadcast.143.clone, s32[64]{0:T(128)S(1)} %copy-done.6, f32[64,3,128]{2,1,0:T(4,128)S(1)} %fusion.60), kind=kCustom, calls=%fused_computation.2 | custom fusion | flops 24576 | bytes 295168 | tf_op jit(solution)/shard_map/scatter-add | solution.py:122
  110.1 2.8 copy.116
  114.7 2.9 %multiply_reduce_fusion.3 = f32[]{:T(128)} fusion(f32[1,16,32,256]{3,2,1,0:T(8,128)} %fusion.15, f32[1,16,32,256]{3,2,1,0:T(8,128)} %get-tuple-element.39, f32[1,16,32,256]{3,2,1,0:T(8,128)} %get-tuple-element.38, f32[3,16,32,256]{3,2,1,0:T(8,128)S(1)} %reshape.212, f32[3,16,32,256]{3,2,1,0:T(8,128)S(1)} %copy-done), kind=kLoop, calls=%fused_computation.14 | loop fusion | flops 3145727 | bytes 4718596 | tf_op jit(solution)/shard_map/reduce_sum | solution.py:133
  118.3 38.0 %psum.28 = f32[]{:T(128)} all-reduce(f32[]{:T(128)} %multiply_reduce_fusion.3), channel_id=1, replica_groups=mesh['radar'=4,'tile'=8] {'radar','tile'}, use_global_device_ids=true, to_apply=%region_3.4 | all-reduce | flops 1 | bytes 8 | tf_op jit(solution)/shard_map/psum | solution.py:132
  157.0 3.2 %multiply_reduce_fusion.1 = (f32[]{:T(128)}, f32[]{:T(128)}, f32[3,16,32,256]{3,2,1,0:T(8,128)S(1)}) fusion(f32[3,16,32,256]{3,2,1,0:T(8,128)S(1)} %copy-done, f32[]{:T(128)S(6)} %sqrt.6, f32[1,16,32,256]{3,2,1,0:T(8,128)} %fusion.15, f32[1,16,32,256]{3,2,1,0:T(8,128)} %get-tuple-element.39, f32[1,16,32,256]{3,2,1,0:T(8,128)} %get-tuple-element.38, ...), kind=kLoop, calls=%fused_computation.10 | loop fusion | flops 5505022 | bytes 6291468 | tf_op jit(solution)/shard_map/reduce_sum | solution.py:129
  170.5 5.1 %collective-permute-start.4 = (f32[3,16,32,2]{2,1,3,0:T(8,128)S(1)}, f32[3,16,32,2]{2,1,3,0:T(8,128)S(1)}, u32[]{:S(2)}, u32[]{:S(2)}) collective-permute-start(f32[3,16,32,2]{2,1,3,0:T(8,128)S(1)} %copy.125), channel_id=1, source_target_pairs={{0,8},{8,16},{16,24},{1,9},{9,17},{17,25},{2,10},{10,18},{18,26},{... | collective-permute-start | bytes 36872 | tf_op jit(solution)/shard_map/ppermute | solution.py:20
  188.4 3.2 %collective-permute-start.6 = (f32[3,2,32,260]{3,2,1,0:T(8,128)}, f32[3,2,32,260]{3,2,1,0:T(8,128)}, u32[]{:S(2)}, u32[]{:S(2)}) collective-permute-start(f32[3,2,32,260]{3,2,1,0:T(8,128)} %get-tuple-element.17), channel_id=1, source_target_pairs={{0,1},{1,2},{2,3},{3,4},{4,5},{5,6},{6,7},{8,9},{9,10},{10,11},{11... | collective-permute-start | bytes 599048 | tf_op jit(solution)/shard_map/ppermute | solution.py:20
  196.9 7.1 %scatter_fusion.1 = f32[3,1024,128]{2,0,1:T(4,128)} fusion(f32[3,1024,128]{2,0,1:T(4,128)} %broadcast.143, s32[64]{0:T(128)S(1)} %copy-done.7, f32[64,3,128]{2,1,0:T(4,128)S(1)} %fusion.58), kind=kCustom, calls=%fused_computation.3 | custom fusion | flops 24576 | bytes 295168 | tf_op jit(solution)/shard_map/scatter-add | solution.py:122
  204.0 2.8 copy.124
  218.3 4.2 %multiply_reduce_fusion.2 = (f32[]{:T(128)}, f32[3,16,32,256]{3,2,1,0:T(8,128)}) fusion(f32[1,16,32,256]{3,2,1,0:T(8,128)} %fusion.19, f32[1,16,32,256]{3,2,1,0:T(8,128)} %get-tuple-element.43, f32[1,16,32,256]{3,2,1,0:T(8,128)} %get-tuple-element.42, f32[3,16,32,256]{3,2,1,0:T(8,128)} %reshape.214, f32[3,16,32,256]{3,2,1,0:T(8,128)S(1)} %get-tuple-element.10, ...), kind=kLoop, calls=%fused_computation.12 | loop fusion | flops 3145727 | bytes 7864324 | tf_op jit(solution)/shard_map/reduce_sum | solution.py:133
  222.5 40.7 %all-reduce.7 = (f32[]{:T(128)}, f32[]{:T(128)}, f32[]{:T(128)}) all-reduce(f32[]{:T(128)} %get-tuple-element.11, f32[]{:T(128)S(6)} %add.135, f32[]{:T(128)S(6)} %add.133), channel_id=1, replica_groups=mesh['radar'=4,'tile'=8] {'radar','tile'}, use_global_device_ids=true, to_apply=%region_7.8 | all-reduce | flops 3 | bytes 24 | tf_op jit(solution)/shard_map/psum | solution.py:132
  266.3 4.9 %collective-permute-start.8 = (f32[3,16,32,1]{2,1,3,0:T(8,128)S(1)}, f32[3,16,32,1]{2,1,3,0:T(8,128)S(1)}, u32[]{:S(2)}, u32[]{:S(2)}) collective-permute-start(f32[3,16,32,1]{2,1,3,0:T(8,128)S(1)} %copy.129), channel_id=1, source_target_pairs={{0,8},{8,16},{16,24},{1,9},{9,17},{17,25},{2,10},{10,18},{18,26},{... | collective-permute-start | bytes 18440 | tf_op jit(solution)/shard_map/ppermute | solution.py:20
  277.3 4.1 %collective-permute-start.10 = (f32[3,1,32,258]{3,2,1,0:T(8,128)S(1)}, f32[3,1,32,258]{3,2,1,0:T(8,128)S(1)}, u32[]{:S(2)}, u32[]{:S(2)}) collective-permute-start(f32[3,1,32,258]{3,2,1,0:T(8,128)S(1)} %get-tuple-element.15), channel_id=1, source_target_pairs={{0,1},{1,2},{2,3},{3,4},{4,5},{5,6},{6,7},{8,9},{9,10},{10,11},{11... | collective-permute-start | bytes 297224 | tf_op jit(solution)/shard_map/ppermute | solution.py:20
  283.3 4.3 %collective-permute-done.11 = f32[3,1,32,258]{3,2,1,0:T(8,128)S(1)} collective-permute-done((f32[3,1,32,258]{3,2,1,0:T(8,128)S(1)}, f32[3,1,32,258]{3,2,1,0:T(8,128)S(1)}, u32[]{:S(2)}, u32[]{:S(2)}) %collective-permute-start.11) | collective-permute-done | bytes 99104 | tf_op jit(solution)/shard_map/ppermute | solution.py:21
  (114 shorter events, 81.7 us)
Async XLA Ops:
  2.8 14.1 %all-to-all-start = ((s32[32,2,2]{2,1,0:T(2,128)}), s32[32,2,2]{2,1,0:T(2,128)S(1)}, u32[]{:S(2)}, u32[]{:S(2)}) async-start(s32[32,2,2]{2,1,0:T(2,128)} %copy.109), calls=%async_computation | async-start | bytes 65536 | tf_op jit(solution)/shard_map/all_to_all | solution.py:86
  25.8 3.5 %copy-start = (f32[3,16,32,256]{3,2,1,0:T(8,128)S(1)}, f32[3,16,32,256]{3,2,1,0:T(8,128)}, u32[]{:S(2)}) copy-start(f32[3,16,32,256]{3,2,1,0:T(8,128)} %param.6) | copy-start | bytes 4718596
  25.8 53.2 %all-to-all-start.2 = ((bf16[32,2,128,128]{3,2,1,0:T(8,128)(2,1)}), bf16[32,2,128,128]{3,2,1,0:T(8,128)(2,1)}, u32[]{:S(2)}, u32[]{:S(2)}) async-start(bf16[32,2,128,128]{3,2,1,0:T(8,128)(2,1)} %bitcast.87), calls=%async_computation.2 | async-start | bytes 4194304 | tf_op jit(solution)/shard_map/all_to_all | solution.py:90
  30.7 10.5 %collective-permute-start = (f32[3,16,32,2]{2,1,3,0:T(8,128)}, f32[3,16,32,2]{2,1,3,0:T(8,128)}, u32[]{:S(2)}, u32[]{:S(2)}) collective-permute-start(f32[3,16,32,2]{2,1,3,0:T(8,128)} %copy.136), channel_id=1, source_target_pairs={{0,8},{8,16},{16,24},{1,9},{9,17},{17,25},{2,10},{10,18},{18,26},{... | collective-permute-start | bytes 36872 | tf_op jit(solution)/shard_map/ppermute | solution.py:20
  35.2 8.0 %collective-permute-start.1 = (f32[3,16,32,2]{2,1,3,0:T(8,128)}, f32[3,16,32,2]{2,1,3,0:T(8,128)}, u32[]{:S(2)}, u32[]{:S(2)}) collective-permute-start(f32[3,16,32,2]{2,1,3,0:T(8,128)} %copy.137), channel_id=1, source_target_pairs={{8,0},{16,8},{24,16},{9,1},{17,9},{25,17},{10,2},{18,10},{26,18},{... | collective-permute-start | bytes 36872 | tf_op jit(solution)/shard_map/ppermute | solution.py:21
  44.6 15.1 %collective-permute-start.2 = (f32[3,2,32,260]{3,2,1,0:T(8,128)S(1)}, f32[3,2,32,260]{3,2,1,0:T(8,128)S(1)}, u32[]{:S(2)}, u32[]{:S(2)}) collective-permute-start(f32[3,2,32,260]{3,2,1,0:T(8,128)S(1)} %get-tuple-element.19), channel_id=1, source_target_pairs={{0,1},{1,2},{2,3},{3,4},{4,5},{5,6},{6,7},{8,9},{9,10},{10,11},{11... | collective-permute-start | bytes 599048 | tf_op jit(solution)/shard_map/ppermute | solution.py:20
  48.0 13.2 %collective-permute-start.3 = (f32[3,2,32,260]{3,2,1,0:T(8,128)S(1)}, f32[3,2,32,260]{3,2,1,0:T(8,128)S(1)}, u32[]{:S(2)}, u32[]{:S(2)}) collective-permute-start(f32[3,2,32,260]{3,2,1,0:T(8,128)S(1)} %get-tuple-element.20), channel_id=1, source_target_pairs={{1,0},{2,1},{3,2},{4,3},{5,4},{6,5},{7,6},{9,8},{10,9},{11,10},{12... | collective-permute-start | bytes 599048 | tf_op jit(solution)/shard_map/ppermute | solution.py:21
  65.6 33.5 %copy-start.8 = (f32[64]{0:T(128)S(1)}, f32[64]{0:T(128)}, u32[]{:S(2)}) copy-start(f32[64]{0:T(128)} %convert_element_type.74) | copy-start | bytes 772
  79.0 20.1 %all-to-all-start.3 = ((bf16[32,2,128]{2,1,0:T(2,128)(2,1)}), bf16[32,2,128]{2,1,0:T(2,128)(2,1)S(1)}, u32[]{:S(2)}, u32[]{:S(2)}) async-start(bf16[32,2,128]{2,1,0:T(2,128)(2,1)} %bitcast.7), calls=%async_computation.3 | async-start | bytes 32768 | tf_op jit(solution)/shard_map/all_to_all | solution.py:104
  99.2 3.8 %copy-start.6 = (s32[64]{0:T(128)S(1)}, s32[64]{0:T(128)}, u32[]{:S(2)}) copy-start(s32[64]{0:T(128)} %copy-done.5) | copy-start | bytes 772
  114.7 3.0 %copy-start.2 = (f32[3,16,32,256]{3,2,1,0:T(8,128)}, f32[3,16,32,256]{3,2,1,0:T(8,128)S(1)}, u32[]{:S(2)}) copy-start(f32[3,16,32,256]{3,2,1,0:T(8,128)S(1)} %reshape.212) | copy-start | bytes 4718596
  161.3 1.4 copy-start.3
  166.2 13.4 %copy-start.9 = (f32[64]{0:T(128)S(1)}, f32[64]{0:T(128)}, u32[]{:S(2)}) copy-start(f32[64]{0:T(128)} %convert_element_type.74) | copy-start | bytes 772
  170.5 12.5 %collective-permute-start.4 = (f32[3,16,32,2]{2,1,3,0:T(8,128)S(1)}, f32[3,16,32,2]{2,1,3,0:T(8,128)S(1)}, u32[]{:S(2)}, u32[]{:S(2)}) collective-permute-start(f32[3,16,32,2]{2,1,3,0:T(8,128)S(1)} %copy.125), channel_id=1, source_target_pairs={{0,8},{8,16},{16,24},{1,9},{9,17},{17,25},{2,10},{10,18},{18,26},{... | collective-permute-start | bytes 36872 | tf_op jit(solution)/shard_map/ppermute | solution.py:20
  177.7 6.5 %collective-permute-start.5 = (f32[3,16,32,2]{2,1,3,0:T(8,128)}, f32[3,16,32,2]{2,1,3,0:T(8,128)}, u32[]{:S(2)}, u32[]{:S(2)}) collective-permute-start(f32[3,16,32,2]{2,1,3,0:T(8,128)} %copy.126), channel_id=1, source_target_pairs={{8,0},{16,8},{24,16},{9,1},{17,9},{25,17},{10,2},{18,10},{26,18},{... | collective-permute-start | bytes 36872 | tf_op jit(solution)/shard_map/ppermute | solution.py:21
  188.4 21.1 %collective-permute-start.6 = (f32[3,2,32,260]{3,2,1,0:T(8,128)}, f32[3,2,32,260]{3,2,1,0:T(8,128)}, u32[]{:S(2)}, u32[]{:S(2)}) collective-permute-start(f32[3,2,32,260]{3,2,1,0:T(8,128)} %get-tuple-element.17), channel_id=1, source_target_pairs={{0,1},{1,2},{2,3},{3,4},{4,5},{5,6},{6,7},{8,9},{9,10},{10,11},{11... | collective-permute-start | bytes 599048 | tf_op jit(solution)/shard_map/ppermute | solution.py:20
  191.6 5.3 %copy-start.7 = (s32[64]{0:T(128)S(1)}, s32[64]{0:T(128)}, u32[]{:S(2)}) copy-start(s32[64]{0:T(128)} %copy-done.5) | copy-start | bytes 772
  191.6 17.9 %collective-permute-start.7 = (f32[3,2,32,260]{3,2,1,0:T(8,128)}, f32[3,2,32,260]{3,2,1,0:T(8,128)}, u32[]{:S(2)}, u32[]{:S(2)}) collective-permute-start(f32[3,2,32,260]{3,2,1,0:T(8,128)} %get-tuple-element.18), channel_id=1, source_target_pairs={{1,0},{2,1},{3,2},{4,3},{5,4},{6,5},{7,6},{9,8},{10,9},{11,10},{12... | collective-permute-start | bytes 599048 | tf_op jit(solution)/shard_map/ppermute | solution.py:21
  265.6 21.9 %copy-start.1 = (f32[3,16,32,256]{3,2,1,0:T(8,128)}, f32[3,16,32,256]{3,2,1,0:T(8,128)S(1)}, u32[]{:S(2)}) copy-start(f32[3,16,32,256]{3,2,1,0:T(8,128)S(1)} %divide_subtract_fusion) | copy-start | bytes 4718596
  266.3 8.5 %collective-permute-start.8 = (f32[3,16,32,1]{2,1,3,0:T(8,128)S(1)}, f32[3,16,32,1]{2,1,3,0:T(8,128)S(1)}, u32[]{:S(2)}, u32[]{:S(2)}) collective-permute-start(f32[3,16,32,1]{2,1,3,0:T(8,128)S(1)} %copy.129), channel_id=1, source_target_pairs={{0,8},{8,16},{16,24},{1,9},{9,17},{17,25},{2,10},{10,18},{18,26},{... | collective-permute-start | bytes 18440 | tf_op jit(solution)/shard_map/ppermute | solution.py:20
  271.6 5.1 %collective-permute-start.9 = (f32[3,16,32,1]{2,1,3,0:T(8,128)S(1)}, f32[3,16,32,1]{2,1,3,0:T(8,128)S(1)}, u32[]{:S(2)}, u32[]{:S(2)}) collective-permute-start(f32[3,16,32,1]{2,1,3,0:T(8,128)S(1)} %copy.130), channel_id=1, source_target_pairs={{8,0},{16,8},{24,16},{9,1},{17,9},{25,17},{10,2},{18,10},{26,18},{... | collective-permute-start | bytes 18440 | tf_op jit(solution)/shard_map/ppermute | solution.py:21
  277.3 6.0 %collective-permute-start.10 = (f32[3,1,32,258]{3,2,1,0:T(8,128)S(1)}, f32[3,1,32,258]{3,2,1,0:T(8,128)S(1)}, u32[]{:S(2)}, u32[]{:S(2)}) collective-permute-start(f32[3,1,32,258]{3,2,1,0:T(8,128)S(1)} %get-tuple-element.15), channel_id=1, source_target_pairs={{0,1},{1,2},{2,3},{3,4},{4,5},{5,6},{6,7},{8,9},{9,10},{10,11},{11... | collective-permute-start | bytes 297224 | tf_op jit(solution)/shard_map/ppermute | solution.py:20
  281.4 6.2 %collective-permute-start.11 = (f32[3,1,32,258]{3,2,1,0:T(8,128)S(1)}, f32[3,1,32,258]{3,2,1,0:T(8,128)S(1)}, u32[]{:S(2)}, u32[]{:S(2)}) collective-permute-start(f32[3,1,32,258]{3,2,1,0:T(8,128)S(1)} %get-tuple-element.16), channel_id=1, source_target_pairs={{1,0},{2,1},{3,2},{4,3},{5,4},{6,5},{7,6},{9,8},{10,9},{11,10},{12... | collective-permute-start | bytes 297224 | tf_op jit(solution)/shard_map/ppermute | solution.py:21
  290.9 1.7 copy-start.4
  (1 other events, 0.6 us)
where the time goes:
time: 294 us; the launch traced here: 293 us
  blocking collectives  87.6 us (30%)
  starting transfers between devices  58 us (20%)
  other arithmetic  46.2 us (16%)
  waiting for transfers between devices  42 us (14%)
  local copies, waits for them, and re-layouts  41 us (14%)
  matrix products  10 us (3%)
  between operations  7.66 us (3%)
    psum x2, blocking collectives, shards(): lax.psum((local_cost, jnp.sum(gradient * gradient)), ('radar', 'tile'))  78.7 us
    ppermute x6, starting transfers between devices, with_halo(): before = lax.ppermute(last, axis, up)  24.3 us
    scatter-add x2, other arithmetic, shards(): obs_cost, obs_flat = (obs_cost, empty.at[:, asked_index, :].add(returned))  14.2 us
    all_to_all x1, starting transfers between devices, shards(): lax.all_to_all(observed.reshape(devices, slots, gate_size), ('radar', 'ti...  13.4 us
    all_to_all x1, waiting for transfers between devices, shards(): lax.all_to_all(interp.reshape(devices, slots, gate_size, gate_size), ('ra...  12.5 us
    ppermute x6, waiting for transfers between devices, with_halo(): before = lax.ppermute(last, axis, up)  11.2 us
    ppermute x6, starting transfers between devices, with_halo(): after = lax.ppermute(first, axis, down)  9.74 us
    all_to_all x1, blocking collectives, shards(): lax.all_to_all(beam.reshape(devices, slots, 3, gate_size), ('radar', 'til...  8.91 us
  transfers between devices with their start and end apart: 15, of which 9 were waited for; matrix products, arithmetic and copies ran while one was open for 13% of the time, Pallas kernels for 0%

commit v1 on v0

--- a/solution.py
+++ b/solution.py
@@ -130,7 +130,7 @@
             + 0.5 * DIVERGENCE_WEIGHT * jnp.sum(spread * spread)
         )
         cost_sum, square_sum = lax.psum(
-            (local_cost, jnp.sum(gradient * gradient)), ("radar", "tile")
+            lax.psum((local_cost, jnp.sum(gradient * gradient)), "tile"), "radar"
         )
         scale = jnp.sqrt(square_sum / total_cells + EPSILON)
         wind_field = wind_field - STEP_LENGTH * gradient / scale

time: 294 us -> 261 us (0.89)
  blocking collectives: 87.6 us -> 60.7 us
  starting transfers between devices: 58 us -> 52.6 us
    psum x2 -> x4, blocking collectives: 78.7 us -> 51.8 us  [the longest x2 31 us: shards(): lax.psum((local_cost, jnp.sum(gradient * gradient)), 'tile')]
    ppermute x6, starting transfers between devices: 24.3 us -> 18.6 us  [with_halo(): before = lax.ppermute(last, axis, up)]
  transfers between devices with their start and end apart: 15 -> 15, of which waited for: 9 -> 9; matrix products, arithmetic and copies ran while one was open for 13% -> 15% of each run, Pallas kernels for 0% -> 0%
where the time goes in v1:
time: 261 us; the launch traced here: 260 us
  blocking collectives  60.7 us (23%)
  starting transfers between devices  52.6 us (20%)
  other arithmetic  46.2 us (18%)
  waiting for transfers between devices  41.5 us (16%)
  local copies, waits for them, and re-layouts  41 us (16%)
  matrix products  10 us (4%)
  between operations  7.66 us (3%)
    psum x2, blocking collectives, shards(): lax.psum((local_cost, jnp.sum(gradient * gradient)), 'tile')  31 us
    psum x2, blocking collectives, shards(): lax.psum(lax.psum((local_cost, jnp.sum(gradient * gradient)), 'tile'), 'r...  20.7 us
    ppermute x6, starting transfers between devices, with_halo(): before = lax.ppermute(last, axis, up)  18.6 us
    scatter-add x2, other arithmetic, shards(): obs_cost, obs_flat = (obs_cost, empty.at[:, asked_index, :].add(returned))  14.2 us
    all_to_all x1, starting transfers between devices, shards(): lax.all_to_all(observed.reshape(devices, slots, gate_size), ('radar', 'ti...  13.4 us
    all_to_all x1, waiting for transfers between devices, shards(): lax.all_to_all(interp.reshape(devices, slots, gate_size, gate_size), ('ra...  12.5 us
    ppermute x6, waiting for transfers between devices, with_halo(): before = lax.ppermute(last, axis, up)  11.2 us
    ppermute x6, starting transfers between devices, with_halo(): after = lax.ppermute(first, axis, down)  9.96 us
  transfers between devices with their start and end apart: 15, of which 9 were waited for; matrix products, arithmetic and copies ran while one was open for 15% of the time, Pallas kernels for 0%

profile of v1, /device:TPU:1, one launch (start us, length us, event | category | flops | bytes accessed | tf_op | source)
XLA Modules:
  0.0 259.8 jit_solution(8950969072427879582)
XLA Ops:
  2.8 7.1 %all-to-all-start = ((s32[32,2,2]{2,1,0:T(2,128)}), s32[32,2,2]{2,1,0:T(2,128)S(1)}, u32[]{:S(2)}, u32[]{:S(2)}) async-start(s32[32,2,2]{2,1,0:T(2,128)} %copy.109), calls=%async_computation | async-start | bytes 65536 | tf_op jit(solution)/shard_map/all_to_all | solution.py:86
  10.7 6.2 %all-to-all-done = s32[32,2,2]{2,1,0:T(2,128)S(1)} async-done(((s32[32,2,2]{2,1,0:T(2,128)}), s32[32,2,2]{2,1,0:T(2,128)S(1)}, u32[]{:S(2)}, u32[]{:S(2)}) %all-to-all-start) | async-done | bytes 544 | tf_op jit(solution)/shard_map/all_to_all | solution.py:86
  16.9 8.9 %all_to_all.20 = bf16[32,2,3,128]{3,1,2,0:T(2,128)(2,1)S(1)} all-to-all(bf16[32,2,3,128]{3,1,2,0:T(2,128)(2,1)S(1)} %copy.110), channel_id=1, replica_groups=mesh['radar'=4,'tile'=8] {'radar','tile'}, dimensions={0} | all-to-all | bytes 98304 | tf_op jit(solution)/shard_map/all_to_all | solution.py:97
  25.8 3.5 %all-to-all-start.2 = ((bf16[32,2,128,128]{3,2,1,0:T(8,128)(2,1)}), bf16[32,2,128,128]{3,2,1,0:T(8,128)(2,1)}, u32[]{:S(2)}, u32[]{:S(2)}) async-start(bf16[32,2,128,128]{3,2,1,0:T(8,128)(2,1)} %bitcast.87), calls=%async_computation.2 | async-start | bytes 4194304 | tf_op jit(solution)/shard_map/all_to_all | solution.py:90
  30.7 3.5 %collective-permute-start = (f32[3,16,32,2]{2,1,3,0:T(8,128)}, f32[3,16,32,2]{2,1,3,0:T(8,128)}, u32[]{:S(2)}, u32[]{:S(2)}) collective-permute-start(f32[3,16,32,2]{2,1,3,0:T(8,128)} %copy.136), channel_id=1, source_target_pairs={{0,8},{8,16},{16,24},{1,9},{9,17},{17,25},{2,10},{10,18},{18,26},{... | collective-permute-start | bytes 36872 | tf_op jit(solution)/shard_map/ppermute | solution.py:20
  44.6 3.4 %collective-permute-start.2 = (f32[3,2,32,260]{3,2,1,0:T(8,128)S(1)}, f32[3,2,32,260]{3,2,1,0:T(8,128)S(1)}, u32[]{:S(2)}, u32[]{:S(2)}) collective-permute-start(f32[3,2,32,260]{3,2,1,0:T(8,128)S(1)} %get-tuple-element.22), channel_id=1, source_target_pairs={{0,1},{1,2},{2,3},{3,4},{4,5},{5,6},{6,7},{8,9},{9,10},{10,11},{11... | collective-permute-start | bytes 599048 | tf_op jit(solution)/shard_map/ppermute | solution.py:20
  49.4 10.3 %collective-permute-done.2 = f32[3,2,32,260]{3,2,1,0:T(8,128)S(1)} collective-permute-done((f32[3,2,32,260]{3,2,1,0:T(8,128)S(1)}, f32[3,2,32,260]{3,2,1,0:T(8,128)S(1)}, u32[]{:S(2)}, u32[]{:S(2)}) %collective-permute-start.2) | collective-permute-done | bytes 199712 | tf_op jit(solution)/shard_map/ppermute | solution.py:20
  66.5 12.5 %all-to-all-done.2 = bf16[32,2,128,128]{3,2,1,0:T(8,128)(2,1)} async-done(((bf16[32,2,128,128]{3,2,1,0:T(8,128)(2,1)}), bf16[32,2,128,128]{3,2,1,0:T(8,128)(2,1)}, u32[]{:S(2)}, u32[]{:S(2)}) %all-to-all-start.2) | async-done | bytes 2097184 | tf_op jit(solution)/shard_map/all_to_all | solution.py:90
  79.0 13.4 %all-to-all-start.3 = ((bf16[32,2,128]{2,1,0:T(2,128)(2,1)}), bf16[32,2,128]{2,1,0:T(2,128)(2,1)S(1)}, u32[]{:S(2)}, u32[]{:S(2)}) async-start(bf16[32,2,128]{2,1,0:T(2,128)(2,1)} %bitcast.7), calls=%async_computation.3 | async-start | bytes 32768 | tf_op jit(solution)/shard_map/all_to_all | solution.py:104
  95.2 3.9 %all-to-all-done.3 = bf16[32,2,128]{2,1,0:T(2,128)(2,1)S(1)} async-done(((bf16[32,2,128]{2,1,0:T(2,128)(2,1)}), bf16[32,2,128]{2,1,0:T(2,128)(2,1)S(1)}, u32[]{:S(2)}, u32[]{:S(2)}) %all-to-all-start.3) | async-done | bytes 16416 | tf_op jit(solution)/shard_map/all_to_all | solution.py:104
  103.0 7.1 %scatter_fusion = f32[3,1024,128]{2,0,1:T(4,128)} fusion(f32[3,1024,128]{2,0,1:T(4,128)} %broadcast.143.clone, s32[64]{0:T(128)S(1)} %copy-done.6, f32[64,3,128]{2,1,0:T(4,128)S(1)} %fusion.60), kind=kCustom, calls=%fused_computation.2 | custom fusion | flops 24576 | bytes 295168 | tf_op jit(solution)/shard_map/scatter-add | solution.py:122
  114.7 2.9 %multiply_reduce_fusion.3 = f32[]{:T(128)} fusion(f32[1,16,32,256]{3,2,1,0:T(8,128)} %fusion.15, f32[1,16,32,256]{3,2,1,0:T(8,128)} %get-tuple-element.42, f32[1,16,32,256]{3,2,1,0:T(8,128)} %get-tuple-element.41, f32[3,16,32,256]{3,2,1,0:T(8,128)S(1)} %reshape.212, f32[3,16,32,256]{3,2,1,0:T(8,128)S(1)} %copy-done), kind=kLoop, calls=%fused_computation.14 | loop fusion | flops 3145727 | bytes 4718596 | tf_op jit(solution)/shard_map/reduce_sum | solution.py:133
  117.7 14.7 %psum.56 = f32[]{:T(128)} all-reduce(f32[]{:T(128)} %multiply_reduce_fusion.3), channel_id=1, replica_groups=mesh['radar'=4,'tile'=8] {'tile'}, use_global_device_ids=true, to_apply=%region_3.4 | all-reduce | flops 1 | bytes 8 | tf_op jit(solution)/shard_map/psum | solution.py:133
  133.0 10.2 %psum.57 = f32[]{:T(128)} all-reduce(f32[]{:T(128)} %psum.56), channel_id=1, replica_groups=mesh['radar'=4,'tile'=8] {'radar'}, use_global_device_ids=true, to_apply=%region_4.5 | all-reduce | flops 1 | bytes 8 | tf_op jit(solution)/shard_map/psum | solution.py:132
  143.9 3.2 %multiply_reduce_fusion.1 = (f32[]{:T(128)}, f32[]{:T(128)}, f32[3,16,32,256]{3,2,1,0:T(8,128)S(1)}) fusion(f32[3,16,32,256]{3,2,1,0:T(8,128)S(1)} %copy-done, f32[]{:T(128)S(6)} %sqrt.6, f32[1,16,32,256]{3,2,1,0:T(8,128)} %fusion.15, f32[1,16,32,256]{3,2,1,0:T(8,128)} %get-tuple-element.42, f32[1,16,32,256]{3,2,1,0:T(8,128)} %get-tuple-element.41, ...), kind=kLoop, calls=%fused_computation.10 | loop fusion | flops 5505022 | bytes 6291468 | tf_op jit(solution)/shard_map/reduce_sum | solution.py:129
  157.4 3.3 %collective-permute-start.4 = (f32[3,16,32,2]{2,1,3,0:T(8,128)S(1)}, f32[3,16,32,2]{2,1,3,0:T(8,128)S(1)}, u32[]{:S(2)}, u32[]{:S(2)}) collective-permute-start(f32[3,16,32,2]{2,1,3,0:T(8,128)S(1)} %copy.125), channel_id=1, source_target_pairs={{0,8},{8,16},{16,24},{1,9},{9,17},{17,25},{2,10},{10,18},{18,26},{... | collective-permute-start | bytes 36872 | tf_op jit(solution)/shard_map/ppermute | solution.py:20
  173.5 3.2 %collective-permute-start.6 = (f32[3,2,32,260]{3,2,1,0:T(8,128)}, f32[3,2,32,260]{3,2,1,0:T(8,128)}, u32[]{:S(2)}, u32[]{:S(2)}) collective-permute-start(f32[3,2,32,260]{3,2,1,0:T(8,128)} %get-tuple-element.20), channel_id=1, source_target_pairs={{0,1},{1,2},{2,3},{3,4},{4,5},{5,6},{6,7},{8,9},{9,10},{10,11},{11... | collective-permute-start | bytes 599048 | tf_op jit(solution)/shard_map/ppermute | solution.py:20
  182.0 7.1 %scatter_fusion.1 = f32[3,1024,128]{2,0,1:T(4,128)} fusion(f32[3,1024,128]{2,0,1:T(4,128)} %broadcast.143, s32[64]{0:T(128)S(1)} %copy-done.7, f32[64,3,128]{2,1,0:T(4,128)S(1)} %fusion.58), kind=kCustom, calls=%fused_computation.3 | custom fusion | flops 24576 | bytes 295168 | tf_op jit(solution)/shard_map/scatter-add | solution.py:122
  189.1 2.8 %copy.124 = f32[3,1024,128]{2,1,0:T(8,128)} copy(f32[3,1024,128]{2,0,1:T(4,128)} %scatter_fusion.1) | data formatting | bytes 3145728 | tf_op jit(solution)/shard_map/scatter-add | solution.py:122
  203.4 4.2 %multiply_reduce_fusion.2 = (f32[]{:T(128)}, f32[3,16,32,256]{3,2,1,0:T(8,128)}) fusion(f32[1,16,32,256]{3,2,1,0:T(8,128)} %fusion.19, f32[1,16,32,256]{3,2,1,0:T(8,128)} %get-tuple-element.46, f32[1,16,32,256]{3,2,1,0:T(8,128)} %get-tuple-element.45, f32[3,16,32,256]{3,2,1,0:T(8,128)} %reshape.214, f32[3,16,32,256]{3,2,1,0:T(8,128)S(1)} %get-tuple-element.13, ...), kind=kLoop, calls=%fused_computation.12 | loop fusion | flops 3145727 | bytes 7864324 | tf_op jit(solution)/shard_map/reduce_sum | solution.py:133
  207.6 16.4 %all-reduce.7 = (f32[]{:T(128)}, f32[]{:T(128)}, f32[]{:T(128)}) all-reduce(f32[]{:T(128)} %get-tuple-element.14, f32[]{:T(128)S(6)} %add.143, f32[]{:T(128)S(6)} %add.141), channel_id=1, replica_groups=mesh['radar'=4,'tile'=8] {'tile'}, use_global_device_ids=true, to_apply=%region_8.9 | all-reduce | flops 3 | bytes 24 | tf_op jit(solution)/shard_map/psum | solution.py:133
  223.9 10.5 %all-reduce.8 = (f32[]{:T(128)}, f32[]{:T(128)}, f32[]{:T(128)}) all-reduce(f32[]{:T(128)} %get-tuple-element.7, f32[]{:T(128)} %get-tuple-element.8, f32[]{:T(128)} %get-tuple-element.9), channel_id=1, replica_groups=mesh['radar'=4,'tile'=8] {'radar'}, use_global_device_ids=true, to_apply=%region_9.10 | all-reduce | flops 3 | bytes 24 | tf_op jit(solution)/shard_map/psum | solution.py:132
  237.6 3.9 %collective-permute-start.8 = (f32[3,16,32,1]{2,1,3,0:T(8,128)S(1)}, f32[3,16,32,1]{2,1,3,0:T(8,128)S(1)}, u32[]{:S(2)}, u32[]{:S(2)}) collective-permute-start(f32[3,16,32,1]{2,1,3,0:T(8,128)S(1)} %copy.129), channel_id=1, source_target_pairs={{0,8},{8,16},{16,24},{1,9},{9,17},{17,25},{2,10},{10,18},{18,26},{... | collective-permute-start | bytes 18440 | tf_op jit(solution)/shard_map/ppermute | solution.py:20
  250.9 3.8 %collective-permute-done.11 = f32[3,1,32,258]{3,2,1,0:T(8,128)S(1)} collective-permute-done((f32[3,1,32,258]{3,2,1,0:T(8,128)S(1)}, f32[3,1,32,258]{3,2,1,0:T(8,128)S(1)}, u32[]{:S(2)}, u32[]{:S(2)}) %collective-permute-start.11) | collective-permute-done | bytes 99104 | tf_op jit(solution)/shard_map/ppermute | solution.py:21
  (116 shorter events, 86.0 us)
Async XLA Ops:
  2.8 14.1 %all-to-all-start = ((s32[32,2,2]{2,1,0:T(2,128)}), s32[32,2,2]{2,1,0:T(2,128)S(1)}, u32[]{:S(2)}, u32[]{:S(2)}) async-start(s32[32,2,2]{2,1,0:T(2,128)} %copy.109), calls=%async_computation | async-start | bytes 65536 | tf_op jit(solution)/shard_map/all_to_all | solution.py:86
  25.8 3.5 %copy-start = (f32[3,16,32,256]{3,2,1,0:T(8,128)S(1)}, f32[3,16,32,256]{3,2,1,0:T(8,128)}, u32[]{:S(2)}) copy-start(f32[3,16,32,256]{3,2,1,0:T(8,128)} %param.6) | copy-start | bytes 4718596
  25.8 53.2 %all-to-all-start.2 = ((bf16[32,2,128,128]{3,2,1,0:T(8,128)(2,1)}), bf16[32,2,128,128]{3,2,1,0:T(8,128)(2,1)}, u32[]{:S(2)}, u32[]{:S(2)}) async-start(bf16[32,2,128,128]{3,2,1,0:T(8,128)(2,1)} %bitcast.87), calls=%async_computation.2 | async-start | bytes 4194304 | tf_op jit(solution)/shard_map/all_to_all | solution.py:90
  30.7 10.5 %collective-permute-start = (f32[3,16,32,2]{2,1,3,0:T(8,128)}, f32[3,16,32,2]{2,1,3,0:T(8,128)}, u32[]{:S(2)}, u32[]{:S(2)}) collective-permute-start(f32[3,16,32,2]{2,1,3,0:T(8,128)} %copy.136), channel_id=1, source_target_pairs={{0,8},{8,16},{16,24},{1,9},{9,17},{17,25},{2,10},{10,18},{18,26},{... | collective-permute-start | bytes 36872 | tf_op jit(solution)/shard_map/ppermute | solution.py:20
  35.2 8.0 %collective-permute-start.1 = (f32[3,16,32,2]{2,1,3,0:T(8,128)}, f32[3,16,32,2]{2,1,3,0:T(8,128)}, u32[]{:S(2)}, u32[]{:S(2)}) collective-permute-start(f32[3,16,32,2]{2,1,3,0:T(8,128)} %copy.137), channel_id=1, source_target_pairs={{8,0},{16,8},{24,16},{9,1},{17,9},{25,17},{10,2},{18,10},{26,18},{... | collective-permute-start | bytes 36872 | tf_op jit(solution)/shard_map/ppermute | solution.py:21
  44.6 15.1 %collective-permute-start.2 = (f32[3,2,32,260]{3,2,1,0:T(8,128)S(1)}, f32[3,2,32,260]{3,2,1,0:T(8,128)S(1)}, u32[]{:S(2)}, u32[]{:S(2)}) collective-permute-start(f32[3,2,32,260]{3,2,1,0:T(8,128)S(1)} %get-tuple-element.22), channel_id=1, source_target_pairs={{0,1},{1,2},{2,3},{3,4},{4,5},{5,6},{6,7},{8,9},{9,10},{10,11},{11... | collective-permute-start | bytes 599048 | tf_op jit(solution)/shard_map/ppermute | solution.py:20
  48.0 13.2 %collective-permute-start.3 = (f32[3,2,32,260]{3,2,1,0:T(8,128)S(1)}, f32[3,2,32,260]{3,2,1,0:T(8,128)S(1)}, u32[]{:S(2)}, u32[]{:S(2)}) collective-permute-start(f32[3,2,32,260]{3,2,1,0:T(8,128)S(1)} %get-tuple-element.23), channel_id=1, source_target_pairs={{1,0},{2,1},{3,2},{4,3},{5,4},{6,5},{7,6},{9,8},{10,9},{11,10},{12... | collective-permute-start | bytes 599048 | tf_op jit(solution)/shard_map/ppermute | solution.py:21
  65.6 33.5 %copy-start.8 = (f32[64]{0:T(128)S(1)}, f32[64]{0:T(128)}, u32[]{:S(2)}) copy-start(f32[64]{0:T(128)} %convert_element_type.74) | copy-start | bytes 772
  79.0 20.1 %all-to-all-start.3 = ((bf16[32,2,128]{2,1,0:T(2,128)(2,1)}), bf16[32,2,128]{2,1,0:T(2,128)(2,1)S(1)}, u32[]{:S(2)}, u32[]{:S(2)}) async-start(bf16[32,2,128]{2,1,0:T(2,128)(2,1)} %bitcast.7), calls=%async_computation.3 | async-start | bytes 32768 | tf_op jit(solution)/shard_map/all_to_all | solution.py:104
  99.2 3.8 %copy-start.6 = (s32[64]{0:T(128)S(1)}, s32[64]{0:T(128)}, u32[]{:S(2)}) copy-start(s32[64]{0:T(128)} %copy-done.5) | copy-start | bytes 772
  114.7 3.0 %copy-start.2 = (f32[3,16,32,256]{3,2,1,0:T(8,128)}, f32[3,16,32,256]{3,2,1,0:T(8,128)S(1)}, u32[]{:S(2)}) copy-start(f32[3,16,32,256]{3,2,1,0:T(8,128)S(1)} %reshape.212) | copy-start | bytes 4718596
  148.2 1.4 copy-start.3
  153.1 11.6 %copy-start.9 = (f32[64]{0:T(128)S(1)}, f32[64]{0:T(128)}, u32[]{:S(2)}) copy-start(f32[64]{0:T(128)} %convert_element_type.74) | copy-start | bytes 772
  157.4 10.7 %collective-permute-start.4 = (f32[3,16,32,2]{2,1,3,0:T(8,128)S(1)}, f32[3,16,32,2]{2,1,3,0:T(8,128)S(1)}, u32[]{:S(2)}, u32[]{:S(2)}) collective-permute-start(f32[3,16,32,2]{2,1,3,0:T(8,128)S(1)} %copy.125), channel_id=1, source_target_pairs={{0,8},{8,16},{16,24},{1,9},{9,17},{17,25},{2,10},{10,18},{18,26},{... | collective-permute-start | bytes 36872 | tf_op jit(solution)/shard_map/ppermute | solution.py:20
  162.8 6.5 %collective-permute-start.5 = (f32[3,16,32,2]{2,1,3,0:T(8,128)}, f32[3,16,32,2]{2,1,3,0:T(8,128)}, u32[]{:S(2)}, u32[]{:S(2)}) collective-permute-start(f32[3,16,32,2]{2,1,3,0:T(8,128)} %copy.126), channel_id=1, source_target_pairs={{8,0},{16,8},{24,16},{9,1},{17,9},{25,17},{10,2},{18,10},{26,18},{... | collective-permute-start | bytes 36872 | tf_op jit(solution)/shard_map/ppermute | solution.py:21
  173.5 21.1 %collective-permute-start.6 = (f32[3,2,32,260]{3,2,1,0:T(8,128)}, f32[3,2,32,260]{3,2,1,0:T(8,128)}, u32[]{:S(2)}, u32[]{:S(2)}) collective-permute-start(f32[3,2,32,260]{3,2,1,0:T(8,128)} %get-tuple-element.20), channel_id=1, source_target_pairs={{0,1},{1,2},{2,3},{3,4},{4,5},{5,6},{6,7},{8,9},{9,10},{10,11},{11... | collective-permute-start | bytes 599048 | tf_op jit(solution)/shard_map/ppermute | solution.py:20
  176.7 5.3 %copy-start.7 = (s32[64]{0:T(128)S(1)}, s32[64]{0:T(128)}, u32[]{:S(2)}) copy-start(s32[64]{0:T(128)} %copy-done.5) | copy-start | bytes 772
  176.7 17.9 %collective-permute-start.7 = (f32[3,2,32,260]{3,2,1,0:T(8,128)}, f32[3,2,32,260]{3,2,1,0:T(8,128)}, u32[]{:S(2)}, u32[]{:S(2)}) collective-permute-start(f32[3,2,32,260]{3,2,1,0:T(8,128)} %get-tuple-element.21), channel_id=1, source_target_pairs={{1,0},{2,1},{3,2},{4,3},{5,4},{6,5},{7,6},{9,8},{10,9},{11,10},{12... | collective-permute-start | bytes 599048 | tf_op jit(solution)/shard_map/ppermute | solution.py:21
  236.9 17.8 %copy-start.1 = (f32[3,16,32,256]{3,2,1,0:T(8,128)}, f32[3,16,32,256]{3,2,1,0:T(8,128)S(1)}, u32[]{:S(2)}) copy-start(f32[3,16,32,256]{3,2,1,0:T(8,128)S(1)} %divide_subtract_fusion) | copy-start | bytes 4718596
  237.6 7.5 %collective-permute-start.8 = (f32[3,16,32,1]{2,1,3,0:T(8,128)S(1)}, f32[3,16,32,1]{2,1,3,0:T(8,128)S(1)}, u32[]{:S(2)}, u32[]{:S(2)}) collective-permute-start(f32[3,16,32,1]{2,1,3,0:T(8,128)S(1)} %copy.129), channel_id=1, source_target_pairs={{0,8},{8,16},{16,24},{1,9},{9,17},{17,25},{2,10},{10,18},{18,26},{... | collective-permute-start | bytes 18440 | tf_op jit(solution)/shard_map/ppermute | solution.py:20
  241.8 5.1 %collective-permute-start.9 = (f32[3,16,32,1]{2,1,3,0:T(8,128)S(1)}, f32[3,16,32,1]{2,1,3,0:T(8,128)S(1)}, u32[]{:S(2)}, u32[]{:S(2)}) collective-permute-start(f32[3,16,32,1]{2,1,3,0:T(8,128)S(1)} %copy.130), channel_id=1, source_target_pairs={{8,0},{16,8},{24,16},{9,1},{17,9},{25,17},{10,2},{18,10},{26,18},{... | collective-permute-start | bytes 18440 | tf_op jit(solution)/shard_map/ppermute | solution.py:21
  247.5 3.4 %collective-permute-start.10 = (f32[3,1,32,258]{3,2,1,0:T(8,128)S(1)}, f32[3,1,32,258]{3,2,1,0:T(8,128)S(1)}, u32[]{:S(2)}, u32[]{:S(2)}) collective-permute-start(f32[3,1,32,258]{3,2,1,0:T(8,128)S(1)} %get-tuple-element.18), channel_id=1, source_target_pairs={{0,1},{1,2},{2,3},{3,4},{4,5},{5,6},{6,7},{8,9},{9,10},{10,11},{11... | collective-permute-start | bytes 297224 | tf_op jit(solution)/shard_map/ppermute | solution.py:20
  248.8 5.9 %collective-permute-start.11 = (f32[3,1,32,258]{3,2,1,0:T(8,128)S(1)}, f32[3,1,32,258]{3,2,1,0:T(8,128)S(1)}, u32[]{:S(2)}, u32[]{:S(2)}) collective-permute-start(f32[3,1,32,258]{3,2,1,0:T(8,128)S(1)} %get-tuple-element.19), channel_id=1, source_target_pairs={{1,0},{2,1},{3,2},{4,3},{5,4},{6,5},{7,6},{9,8},{10,9},{11,10},{12... | collective-permute-start | bytes 297224 | tf_op jit(solution)/shard_map/ppermute | solution.py:21
  258.1 1.7 copy-start.4
  (1 other events, 0.6 us)
